TPU v7x, 32 devices: a whole 2x2x4 slice. The times are simulated.
32 devices in a mesh: wide: 8 (over z, y), narrow: 4 (over x, core).
Axes of the slice: x: 2, y: 2, z: 4, core: 2. Of those that a mesh axis runs over, the one named last changes fastest.
Arguments:
- checkpoint_slots: float32 [4, 2, 256, 4096], P('narrow', None, 'wide'), may hold values from 0 to 2
- owner_slot: int32 [2], replicated, may hold values from 0 to 3
- row_velocity: float32 [256, 4096], P('wide', 'narrow'), may hold values from -0.4 to 0.4
- column_velocity: float32 [256, 4096], P('wide', 'narrow'), may hold values from -0.4 to 0.4
- land_sea: int32 [256, 4096], P('wide', 'narrow'), may hold values 0 or 1
- layer_class: int32 [2], replicated, may hold values from 0 to 3
- class_speed: float32 [4], replicated, may hold values from 0.05 to 0.6
- final_adjoint: float32 [2, 256, 4096], P(None, 'wide', 'narrow'), may hold values from -6 to 6
- deposit_weight: float32 [256, 4096], P('wide', 'narrow'), may hold values from -6 to 6
Outputs:
- initial_adjoint: float32 [2, 256, 4096], P(None, 'wide', 'narrow')
All inputs are finite; a program needn't handle non-finite values. No bound on the sum of `land_sea` on one device may be relied on, other than what follows from the above.
Results may differ from a plain program's by a relative error of at most 0.00002.
Values sent between devices are 32-bit elements; how exact they have to be, the bound alone decides.
A program may use at most 64 MiB of HBM per device.

v0:
```python
import jax
import jax.numpy as jnp
from jax import lax
from jax.sharding import PartitionSpec as P

STEPS = 3


def passed_along(value, axis, by):
    peers = lax.axis_size(axis)
    return lax.ppermute(value, axis, [(i, (i + by) % peers) for i in range(peers)])


def extended(cells, sides, width):
    for axis, dim in sides:
        count = lax.axis_size(axis)
        ends = count - 1
        head = lax.slice_in_dim(cells, 0, width, axis=dim)
        tail = lax.slice_in_dim(cells, cells.shape[dim] - width, cells.shape[dim], axis=dim)
        cells = jnp.concatenate(
            [
                lax.ppermute(tail, axis, [(i, (i + 1) % count) for i in range(ends)]),
                cells,
                lax.ppermute(head, axis, [((i + 1) % count, i) for i in range(ends)]),
            ],
            axis=dim,
        )
    return cells


def stencil_weights(velocity):
    forward_part = jnp.maximum(velocity, 0.0)
    backward_part = jnp.minimum(velocity, 0.0)
    fsquare = forward_part * forward_part
    bsquare = backward_part * backward_part
    return [
        0.5 * fsquare - 0.5 * forward_part,
        2.0 * forward_part - fsquare,
        0.5 * fsquare - 1.5 * forward_part + 0.5 * bsquare + 1.5 * backward_part,
        -2.0 * backward_part - bsquare,
        0.5 * bsquare + 0.5 * backward_part,
    ]


def advect(padded, row_weights, column_weights):
    height = padded.shape[1]
    breadth = padded.shape[2]
    result = padded[:, 2 : height - 2, 2 : breadth - 2]
    for offset in range(-2, 3):
        row_term = row_weights[offset + 2][2 : height - 2, 2 : breadth - 2]
        column_term = column_weights[offset + 2][2 : height - 2, 2 : breadth - 2]
        result = result + row_term * padded[:, 2 + offset : height - 2 + offset, 2 : breadth - 2]
        result = result + column_term * padded[:, 2 : height - 2, 2 + offset : breadth - 2 + offset]
    return result


def transpose_advect(padded, row_weights, column_weights):
    height = padded.shape[1]
    breadth = padded.shape[2]
    result = padded[:, 2 : height - 2, 2 : breadth - 2]
    for offset in range(-2, 3):
        row_term = row_weights[offset + 2][2 - offset : height - 2 - offset, 2 : breadth - 2]
        column_term = column_weights[offset + 2][2 : height - 2, 2 - offset : breadth - 2 - offset]
        result = result + row_term * padded[:, 2 - offset : height - 2 - offset, 2 : breadth - 2]
        result = result + column_term * padded[:, 2 : height - 2, 2 - offset : breadth - 2 - offset]
    return result


def settle(advected, speeds, sea_mask):
    flux = speeds[:, None, None] * advected / (1.0 + advected * advected)
    above = jnp.concatenate([jnp.zeros_like(flux[:1]), flux[:-1]], 0)
    return (advected - flux + above) * sea_mask


def weights_of(flow_now):
    return (stencil_weights(flow_now[0]), stencil_weights(flow_now[1]))


def body(
    checkpoint_slots,
    owner_slot,
    row_velocity,
    column_velocity,
    land_sea,
    layer_class,
    class_speed,
    final_adjoint,
    deposit_weight,
):
    columns = row_velocity.shape[1]
    group = lax.axis_size("narrow")
    here = lax.axis_index("narrow")
    own_slot = checkpoint_slots[0]
    own_block = lax.dynamic_slice_in_dim(own_slot, here * columns, columns, 2)
    start_state = jnp.where(
        (owner_slot == here)[:, None, None], own_block, jnp.zeros_like(own_block)
    )
    for distance in range(1, group):
        target = (here + distance) % group
        outgoing = lax.dynamic_slice_in_dim(own_slot, target * columns, columns, 2)
        incoming = passed_along(outgoing, "narrow", distance)
        sender = (here - distance + group) % group
        start_state = jnp.where((owner_slot == sender)[:, None, None], incoming, start_state)
    classes = jnp.arange(class_speed.shape[0], dtype=jnp.int32)
    speeds = jnp.sum(
        jnp.where(layer_class[:, None] == classes[None, :], class_speed[None, :], 0.0), axis=1
    )
    sea_mask = land_sea.astype(jnp.float32)
    rim_width = 2
    flow_fields = jnp.stack([row_velocity, column_velocity, sea_mask])
    padded_flow = extended(flow_fields, (("wide", 1), ("narrow", 2)), rim_width)
    advected_list = []
    row_weights, column_weights = weights_of(padded_flow)
    current = start_state
    for step_index in range(STEPS):
        padded = extended(current, (("wide", 1), ("narrow", 2)), 2)
        advected = advect(padded, row_weights, column_weights)
        advected_list.append(advected)
        if step_index + 1 < STEPS:
            current = settle(advected, speeds, sea_mask)
    row_weights, column_weights = weights_of(padded_flow)
    bottom_weight = (sea_mask * deposit_weight)[None]
    adjoint = final_adjoint
    for step_index in reversed(range(STEPS)):
        advected = advected_list[step_index]
        masked = adjoint * sea_mask
        below = jnp.concatenate([masked[1:], jnp.zeros_like(masked[:1])], 0)
        flux_grad = (
            below - masked + jnp.concatenate([jnp.zeros_like(masked[:-1]), bottom_weight], 0)
        )
        square = advected * advected
        slope = speeds[:, None, None] * (1.0 - square) / ((1.0 + square) * (1.0 + square))
        grad_adv = masked + flux_grad * slope
        padded_grad = extended(grad_adv, (("wide", 1), ("narrow", 2)), 2)
        adjoint = transpose_advect(padded_grad, row_weights, column_weights)
    return adjoint


def solution(mesh):
    in_specs = (
        P("narrow", None, "wide", None),
        P(),
        P("wide", "narrow"),
        P("wide", "narrow"),
        P("wide", "narrow"),
        P(),
        P(),
        P(None, "wide", "narrow"),
        P("wide", "narrow"),
    )
    out_specs = P(None, "wide", "narrow")
    return jax.shard_map(body, mesh=mesh, in_specs=in_specs, out_specs=out_specs, check_vma=False)
```

profile of v0, /device:TPU:18, one launch (start us, length us, event | category | flops | bytes accessed | tf_op | source)
XLA Modules:
  0.0 133.5 jit_solution(8760613477783485825)
XLA Ops:
  1.1 3.4 %collective-permute-start.3 = (f32[3,2,1024]{2,1,0:T(2,128)S(1)}, f32[3,2,1024]{2,1,0:T(2,128)S(1)}, u32[]{:S(2)}, u32[]{:S(2)}) collective-permute-start(f32[3,2,1024]{2,1,0:T(2,128)S(1)} %get-tuple-element.24), channel_id=1, source_target_pairs={{0,4},{4,8},{8,12},{12,16},{16,20},{20,24},{24,28},{1,5},{5,9},{9,... | collective-permute-start | bytes 73736 | tf_op jit(solution)/shard_map/ppermute | solution.py:22
  4.5 3.3 %collective-permute-start.4 = (f32[3,2,1024]{2,1,0:T(2,128)S(1)}, f32[3,2,1024]{2,1,0:T(2,128)S(1)}, u32[]{:S(2)}, u32[]{:S(2)}) collective-permute-start(f32[3,2,1024]{2,1,0:T(2,128)S(1)} %get-tuple-element.25), channel_id=1, source_target_pairs={{4,0},{8,4},{12,8},{16,12},{20,16},{24,20},{28,24},{5,1},{9,5},{13... | collective-permute-start | bytes 73736 | tf_op jit(solution)/shard_map/ppermute | solution.py:24
  11.3 2.4 %collective-permute-start.6 = (f32[3,36,2]{2,1,0:T(8,128)S(1)}, f32[3,36,2]{2,1,0:T(8,128)S(1)}, u32[]{:S(2)}, u32[]{:S(2)}) collective-permute-start(f32[3,36,2]{2,1,0:T(8,128)S(1)} %get-tuple-element.22), channel_id=1, source_target_pairs={{1,0},{2,1},{3,2},{5,4},{6,5},{7,6},{9,8},{10,9},{11,10},{13,12},{... | collective-permute-start | bytes 2600 | tf_op jit(solution)/shard_map/ppermute | solution.py:24
  16.0 6.1 %collective-permute-done.6 = f32[3,36,2]{2,1,0:T(8,128)S(1)} collective-permute-done((f32[3,36,2]{2,1,0:T(8,128)S(1)}, f32[3,36,2]{2,1,0:T(8,128)S(1)}, u32[]{:S(2)}, u32[]{:S(2)}) %collective-permute-start.6) | collective-permute-done | bytes 896 | tf_op jit(solution)/shard_map/ppermute | solution.py:24
  26.1 2.5 %collective-permute-start.7 = (f32[2,2,1024]{2,1,0:T(2,128)S(1)}, f32[2,2,1024]{2,1,0:T(2,128)S(1)}, u32[]{:S(2)}, u32[]{:S(2)}) collective-permute-start(f32[2,2,1024]{2,1,0:T(2,128)S(1)} %get-tuple-element.60), channel_id=1, source_target_pairs={{0,4},{4,8},{8,12},{12,16},{16,20},{20,24},{24,28},{1,5},{5,9},{9,... | collective-permute-start | bytes 49160 | tf_op jit(solution)/shard_map/ppermute | solution.py:22
  28.6 4.2 %collective-permute-start.8 = (f32[2,2,1024]{2,1,0:T(2,128)S(1)}, f32[2,2,1024]{2,1,0:T(2,128)S(1)}, u32[]{:S(2)}, u32[]{:S(2)}) collective-permute-start(f32[2,2,1024]{2,1,0:T(2,128)S(1)} %get-tuple-element.61), channel_id=1, source_target_pairs={{4,0},{8,4},{12,8},{16,12},{20,16},{24,20},{28,24},{5,1},{9,5},{13... | collective-permute-start | bytes 49160 | tf_op jit(solution)/shard_map/ppermute | solution.py:24
  36.7 3.6 %collective-permute-start.10 = (f32[2,36,2]{2,1,0:T(8,128)S(1)}, f32[2,36,2]{2,1,0:T(8,128)S(1)}, u32[]{:S(2)}, u32[]{:S(2)}) collective-permute-start(f32[2,36,2]{2,1,0:T(8,128)S(1)} %get-tuple-element.49), channel_id=1, source_target_pairs={{1,0},{2,1},{3,2},{5,4},{6,5},{7,6},{9,8},{10,9},{11,10},{13,12},{... | collective-permute-start | bytes 1736 | tf_op jit(solution)/shard_map/ppermute | solution.py:24
  42.8 4.8 %collective-permute-start.11 = (f32[2,2,1024]{2,1,0:T(2,128)S(1)}, f32[2,2,1024]{2,1,0:T(2,128)S(1)}, u32[]{:S(2)}, u32[]{:S(2)}) collective-permute-start(f32[2,2,1024]{2,1,0:T(2,128)S(1)} %get-tuple-element.58), channel_id=1, source_target_pairs={{0,4},{4,8},{8,12},{12,16},{16,20},{20,24},{24,28},{1,5},{5,9},{9,... | collective-permute-start | bytes 49160 | tf_op jit(solution)/shard_map/ppermute | solution.py:22
  49.6 3.7 %collective-permute-done.12 = f32[2,2,1024]{2,1,0:T(2,128)S(1)} collective-permute-done((f32[2,2,1024]{2,1,0:T(2,128)S(1)}, f32[2,2,1024]{2,1,0:T(2,128)S(1)}, u32[]{:S(2)}, u32[]{:S(2)}) %collective-permute-start.12) | collective-permute-done | bytes 16416 | tf_op jit(solution)/shard_map/ppermute | solution.py:24
  55.3 3.6 %collective-permute-start.14 = (f32[2,36,2]{2,1,0:T(8,128)S(1)}, f32[2,36,2]{2,1,0:T(8,128)S(1)}, u32[]{:S(2)}, u32[]{:S(2)}) collective-permute-start(f32[2,36,2]{2,1,0:T(8,128)S(1)} %get-tuple-element.45), channel_id=1, source_target_pairs={{1,0},{2,1},{3,2},{5,4},{6,5},{7,6},{9,8},{10,9},{11,10},{13,12},{... | collective-permute-start | bytes 1736 | tf_op jit(solution)/shard_map/ppermute | solution.py:24
  62.3 2.8 %collective-permute-start.15 = (f32[2,2,1024]{2,1,0:T(2,128)S(1)}, f32[2,2,1024]{2,1,0:T(2,128)S(1)}, u32[]{:S(2)}, u32[]{:S(2)}) collective-permute-start(f32[2,2,1024]{2,1,0:T(2,128)S(1)} %get-tuple-element.56), channel_id=1, source_target_pairs={{0,4},{4,8},{8,12},{12,16},{16,20},{20,24},{24,28},{1,5},{5,9},{9,... | collective-permute-start | bytes 49160 | tf_op jit(solution)/shard_map/ppermute | solution.py:22
  65.2 4.1 %collective-permute-start.16 = (f32[2,2,1024]{2,1,0:T(2,128)S(1)}, f32[2,2,1024]{2,1,0:T(2,128)S(1)}, u32[]{:S(2)}, u32[]{:S(2)}) collective-permute-start(f32[2,2,1024]{2,1,0:T(2,128)S(1)} %get-tuple-element.57), channel_id=1, source_target_pairs={{4,0},{8,4},{12,8},{16,12},{20,16},{24,20},{28,24},{5,1},{9,5},{13... | collective-permute-start | bytes 49160 | tf_op jit(solution)/shard_map/ppermute | solution.py:24
  72.9 3.6 %collective-permute-start.18 = (f32[2,36,2]{2,1,0:T(8,128)S(1)}, f32[2,36,2]{2,1,0:T(8,128)S(1)}, u32[]{:S(2)}, u32[]{:S(2)}) collective-permute-start(f32[2,36,2]{2,1,0:T(8,128)S(1)} %get-tuple-element.41), channel_id=1, source_target_pairs={{1,0},{2,1},{3,2},{5,4},{6,5},{7,6},{9,8},{10,9},{11,10},{13,12},{... | collective-permute-start | bytes 1736 | tf_op jit(solution)/shard_map/ppermute | solution.py:24
  79.0 4.8 %collective-permute-start.19 = (f32[2,2,1024]{2,1,0:T(2,128)S(1)}, f32[2,2,1024]{2,1,0:T(2,128)S(1)}, u32[]{:S(2)}, u32[]{:S(2)}) collective-permute-start(f32[2,2,1024]{2,1,0:T(2,128)S(1)} %get-tuple-element.54), channel_id=1, source_target_pairs={{4,0},{8,4},{12,8},{16,12},{20,16},{24,20},{28,24},{5,1},{9,5},{13... | collective-permute-start | bytes 49160 | tf_op jit(solution)/shard_map/ppermute | solution.py:24
  85.7 4.6 %collective-permute-done.20 = f32[2,2,1024]{2,1,0:T(2,128)S(1)} collective-permute-done((f32[2,2,1024]{2,1,0:T(2,128)S(1)}, f32[2,2,1024]{2,1,0:T(2,128)S(1)}, u32[]{:S(2)}, u32[]{:S(2)}) %collective-permute-start.20) | collective-permute-done | bytes 16416 | tf_op jit(solution)/shard_map/ppermute | solution.py:22
  94.8 3.2 %collective-permute-done.22 = f32[2,36,2]{2,1,0:T(8,128)S(1)} collective-permute-done((f32[2,36,2]{2,1,0:T(8,128)S(1)}, f32[2,36,2]{2,1,0:T(8,128)S(1)}, u32[]{:S(2)}, u32[]{:S(2)}) %collective-permute-start.22) | collective-permute-done | bytes 608 | tf_op jit(solution)/shard_map/ppermute | solution.py:22
  100.7 3.9 %collective-permute-start.24 = (f32[2,2,1024]{2,1,0:T(2,128)S(1)}, f32[2,2,1024]{2,1,0:T(2,128)S(1)}, u32[]{:S(2)}, u32[]{:S(2)}) collective-permute-start(f32[2,2,1024]{2,1,0:T(2,128)S(1)} %get-tuple-element.53), channel_id=1, source_target_pairs={{0,4},{4,8},{8,12},{12,16},{16,20},{20,24},{24,28},{1,5},{5,9},{9,... | collective-permute-start | bytes 49160 | tf_op jit(solution)/shard_map/ppermute | solution.py:22
  104.6 2.6 %collective-permute-done.24 = f32[2,2,1024]{2,1,0:T(2,128)S(1)} collective-permute-done((f32[2,2,1024]{2,1,0:T(2,128)S(1)}, f32[2,2,1024]{2,1,0:T(2,128)S(1)}, u32[]{:S(2)}, u32[]{:S(2)}) %collective-permute-start.24) | collective-permute-done | bytes 16416 | tf_op jit(solution)/shard_map/ppermute | solution.py:22
  109.3 2.4 %collective-permute-start.26 = (f32[2,36,2]{2,1,0:T(8,128)S(1)}, f32[2,36,2]{2,1,0:T(8,128)S(1)}, u32[]{:S(2)}, u32[]{:S(2)}) collective-permute-start(f32[2,36,2]{2,1,0:T(8,128)S(1)} %get-tuple-element.33), channel_id=1, source_target_pairs={{0,1},{1,2},{2,3},{4,5},{5,6},{6,7},{8,9},{9,10},{10,11},{12,13},{... | collective-permute-start | bytes 1736 | tf_op jit(solution)/shard_map/ppermute | solution.py:22
  111.7 2.9 %collective-permute-done.26 = f32[2,36,2]{2,1,0:T(8,128)S(1)} collective-permute-done((f32[2,36,2]{2,1,0:T(8,128)S(1)}, f32[2,36,2]{2,1,0:T(8,128)S(1)}, u32[]{:S(2)}, u32[]{:S(2)}) %collective-permute-start.26) | collective-permute-done | bytes 608 | tf_op jit(solution)/shard_map/ppermute | solution.py:22
  115.4 2.9 %collective-permute-start.27 = (f32[2,2,1024]{2,1,0:T(2,128)S(1)}, f32[2,2,1024]{2,1,0:T(2,128)S(1)}, u32[]{:S(2)}, u32[]{:S(2)}) collective-permute-start(f32[2,2,1024]{2,1,0:T(2,128)S(1)} %get-tuple-element.50), channel_id=1, source_target_pairs={{4,0},{8,4},{12,8},{16,12},{20,16},{24,20},{28,24},{5,1},{9,5},{13... | collective-permute-start | bytes 49160 | tf_op jit(solution)/shard_map/ppermute | solution.py:24
  118.3 2.9 %collective-permute-start.28 = (f32[2,2,1024]{2,1,0:T(2,128)S(1)}, f32[2,2,1024]{2,1,0:T(2,128)S(1)}, u32[]{:S(2)}, u32[]{:S(2)}) collective-permute-start(f32[2,2,1024]{2,1,0:T(2,128)S(1)} %get-tuple-element.51), channel_id=1, source_target_pairs={{0,4},{4,8},{8,12},{12,16},{16,20},{20,24},{24,28},{1,5},{5,9},{9,... | collective-permute-start | bytes 49160 | tf_op jit(solution)/shard_map/ppermute | solution.py:22
  121.3 3.6 %collective-permute-done.28 = f32[2,2,1024]{2,1,0:T(2,128)S(1)} collective-permute-done((f32[2,2,1024]{2,1,0:T(2,128)S(1)}, f32[2,2,1024]{2,1,0:T(2,128)S(1)}, u32[]{:S(2)}, u32[]{:S(2)}) %collective-permute-start.28) | collective-permute-done | bytes 16416 | tf_op jit(solution)/shard_map/ppermute | solution.py:22
  129.3 2.9 %collective-permute-done.30 = f32[2,36,2]{2,1,0:T(8,128)S(1)} collective-permute-done((f32[2,36,2]{2,1,0:T(8,128)S(1)}, f32[2,36,2]{2,1,0:T(8,128)S(1)}, u32[]{:S(2)}, u32[]{:S(2)}) %collective-permute-start.30) | collective-permute-done | bytes 608 | tf_op jit(solution)/shard_map/ppermute | solution.py:22
  (104 shorter events, 47.7 us)
Async XLA Ops:
  1.1 10.1 %collective-permute-start.3 = (f32[3,2,1024]{2,1,0:T(2,128)S(1)}, f32[3,2,1024]{2,1,0:T(2,128)S(1)}, u32[]{:S(2)}, u32[]{:S(2)}) collective-permute-start(f32[3,2,1024]{2,1,0:T(2,128)S(1)} %get-tuple-element.24), channel_id=1, source_target_pairs={{0,4},{4,8},{8,12},{12,16},{16,20},{20,24},{24,28},{1,5},{5,9},{9,... | collective-permute-start | bytes 73736 | tf_op jit(solution)/shard_map/ppermute | solution.py:22
  4.5 6.6 %collective-permute-start.4 = (f32[3,2,1024]{2,1,0:T(2,128)S(1)}, f32[3,2,1024]{2,1,0:T(2,128)S(1)}, u32[]{:S(2)}, u32[]{:S(2)}) collective-permute-start(f32[3,2,1024]{2,1,0:T(2,128)S(1)} %get-tuple-element.25), channel_id=1, source_target_pairs={{4,0},{8,4},{12,8},{16,12},{20,16},{24,20},{28,24},{5,1},{9,5},{13... | collective-permute-start | bytes 73736 | tf_op jit(solution)/shard_map/ppermute | solution.py:24
  9.0 15.9 %collective-permute-start.2 = (f32[2,32,1024]{2,1,0:T(8,128)S(1)}, f32[2,32,1024]{2,1,0:T(8,128)S(1)}, u32[]{:S(2)}, u32[]{:S(2)}) collective-permute-start(f32[2,32,1024]{2,1,0:T(8,128)S(1)} %get-tuple-element.9), channel_id=1, source_target_pairs={{0,1},{1,2},{2,3},{3,0},{4,5},{5,6},{6,7},{7,4},{8,9},{9,10},{10,1... | collective-permute-start | bytes 786440 | tf_op jit(solution)/shard_map/ppermute | solution.py:11
  9.1 15.8 %collective-permute-start.1 = (f32[2,32,1024]{2,1,0:T(8,128)S(1)}, f32[2,32,1024]{2,1,0:T(8,128)S(1)}, u32[]{:S(2)}, u32[]{:S(2)}) collective-permute-start(f32[2,32,1024]{2,1,0:T(8,128)S(1)} %get-tuple-element.10), channel_id=1, source_target_pairs={{0,2},{1,3},{2,0},{3,1},{4,6},{5,7},{6,4},{7,5},{8,10},{9,11},{10,... | collective-permute-start | bytes 786440 | tf_op jit(solution)/shard_map/ppermute | solution.py:11
  9.7 15.3 %collective-permute-start = (f32[2,32,1024]{2,1,0:T(8,128)S(1)}, f32[2,32,1024]{2,1,0:T(8,128)S(1)}, u32[]{:S(2)}, u32[]{:S(2)}) collective-permute-start(f32[2,32,1024]{2,1,0:T(8,128)S(1)} %get-tuple-element.11), channel_id=1, source_target_pairs={{0,3},{1,0},{2,1},{3,2},{4,7},{5,4},{6,5},{7,6},{8,11},{9,8},{10,9... | collective-permute-start | bytes 786440 | tf_op jit(solution)/shard_map/ppermute | solution.py:11
  11.3 10.7 %collective-permute-start.6 = (f32[3,36,2]{2,1,0:T(8,128)S(1)}, f32[3,36,2]{2,1,0:T(8,128)S(1)}, u32[]{:S(2)}, u32[]{:S(2)}) collective-permute-start(f32[3,36,2]{2,1,0:T(8,128)S(1)} %get-tuple-element.22), channel_id=1, source_target_pairs={{1,0},{2,1},{3,2},{5,4},{6,5},{7,6},{9,8},{10,9},{11,10},{13,12},{... | collective-permute-start | bytes 2600 | tf_op jit(solution)/shard_map/ppermute | solution.py:24
  13.7 10.2 %collective-permute-start.5 = (f32[3,36,2]{2,1,0:T(8,128)S(1)}, f32[3,36,2]{2,1,0:T(8,128)S(1)}, u32[]{:S(2)}, u32[]{:S(2)}) collective-permute-start(f32[3,36,2]{2,1,0:T(8,128)S(1)} %get-tuple-element.23), channel_id=1, source_target_pairs={{0,1},{1,2},{2,3},{4,5},{5,6},{6,7},{8,9},{9,10},{10,11},{12,13},{... | collective-permute-start | bytes 2600 | tf_op jit(solution)/shard_map/ppermute | solution.py:22
  26.1 7.0 %collective-permute-start.7 = (f32[2,2,1024]{2,1,0:T(2,128)S(1)}, f32[2,2,1024]{2,1,0:T(2,128)S(1)}, u32[]{:S(2)}, u32[]{:S(2)}) collective-permute-start(f32[2,2,1024]{2,1,0:T(2,128)S(1)} %get-tuple-element.60), channel_id=1, source_target_pairs={{0,4},{4,8},{8,12},{12,16},{16,20},{20,24},{24,28},{1,5},{5,9},{9,... | collective-permute-start | bytes 49160 | tf_op jit(solution)/shard_map/ppermute | solution.py:22
  28.6 6.0 %collective-permute-start.8 = (f32[2,2,1024]{2,1,0:T(2,128)S(1)}, f32[2,2,1024]{2,1,0:T(2,128)S(1)}, u32[]{:S(2)}, u32[]{:S(2)}) collective-permute-start(f32[2,2,1024]{2,1,0:T(2,128)S(1)} %get-tuple-element.61), channel_id=1, source_target_pairs={{4,0},{8,4},{12,8},{16,12},{20,16},{24,20},{28,24},{5,1},{9,5},{13... | collective-permute-start | bytes 49160 | tf_op jit(solution)/shard_map/ppermute | solution.py:24
  34.8 6.0 %collective-permute-start.9 = (f32[2,36,2]{2,1,0:T(8,128)S(1)}, f32[2,36,2]{2,1,0:T(8,128)S(1)}, u32[]{:S(2)}, u32[]{:S(2)}) collective-permute-start(f32[2,36,2]{2,1,0:T(8,128)S(1)} %get-tuple-element.48), channel_id=1, source_target_pairs={{0,1},{1,2},{2,3},{4,5},{5,6},{6,7},{8,9},{9,10},{10,11},{12,13},{... | collective-permute-start | bytes 1736 | tf_op jit(solution)/shard_map/ppermute | solution.py:22
  42.8 6.8 %collective-permute-start.11 = (f32[2,2,1024]{2,1,0:T(2,128)S(1)}, f32[2,2,1024]{2,1,0:T(2,128)S(1)}, u32[]{:S(2)}, u32[]{:S(2)}) collective-permute-start(f32[2,2,1024]{2,1,0:T(2,128)S(1)} %get-tuple-element.58), channel_id=1, source_target_pairs={{0,4},{4,8},{8,12},{12,16},{16,20},{20,24},{24,28},{1,5},{5,9},{9,... | collective-permute-start | bytes 49160 | tf_op jit(solution)/shard_map/ppermute | solution.py:22
  47.6 5.6 %collective-permute-start.12 = (f32[2,2,1024]{2,1,0:T(2,128)S(1)}, f32[2,2,1024]{2,1,0:T(2,128)S(1)}, u32[]{:S(2)}, u32[]{:S(2)}) collective-permute-start(f32[2,2,1024]{2,1,0:T(2,128)S(1)} %get-tuple-element.59), channel_id=1, source_target_pairs={{4,0},{8,4},{12,8},{16,12},{20,16},{24,20},{28,24},{5,1},{9,5},{13... | collective-permute-start | bytes 49160 | tf_op jit(solution)/shard_map/ppermute | solution.py:24
  53.3 5.6 %collective-permute-start.13 = (f32[2,36,2]{2,1,0:T(8,128)S(1)}, f32[2,36,2]{2,1,0:T(8,128)S(1)}, u32[]{:S(2)}, u32[]{:S(2)}) collective-permute-start(f32[2,36,2]{2,1,0:T(8,128)S(1)} %get-tuple-element.44), channel_id=1, source_target_pairs={{0,1},{1,2},{2,3},{4,5},{5,6},{6,7},{8,9},{9,10},{10,11},{12,13},{... | collective-permute-start | bytes 1736 | tf_op jit(solution)/shard_map/ppermute | solution.py:22
  62.3 6.9 %collective-permute-start.15 = (f32[2,2,1024]{2,1,0:T(2,128)S(1)}, f32[2,2,1024]{2,1,0:T(2,128)S(1)}, u32[]{:S(2)}, u32[]{:S(2)}) collective-permute-start(f32[2,2,1024]{2,1,0:T(2,128)S(1)} %get-tuple-element.56), channel_id=1, source_target_pairs={{0,4},{4,8},{8,12},{12,16},{16,20},{20,24},{24,28},{1,5},{5,9},{9,... | collective-permute-start | bytes 49160 | tf_op jit(solution)/shard_map/ppermute | solution.py:22
  65.2 5.8 %collective-permute-start.16 = (f32[2,2,1024]{2,1,0:T(2,128)S(1)}, f32[2,2,1024]{2,1,0:T(2,128)S(1)}, u32[]{:S(2)}, u32[]{:S(2)}) collective-permute-start(f32[2,2,1024]{2,1,0:T(2,128)S(1)} %get-tuple-element.57), channel_id=1, source_target_pairs={{4,0},{8,4},{12,8},{16,12},{20,16},{24,20},{28,24},{5,1},{9,5},{13... | collective-permute-start | bytes 49160 | tf_op jit(solution)/shard_map/ppermute | solution.py:24
  71.0 5.6 %collective-permute-start.17 = (f32[2,36,2]{2,1,0:T(8,128)S(1)}, f32[2,36,2]{2,1,0:T(8,128)S(1)}, u32[]{:S(2)}, u32[]{:S(2)}) collective-permute-start(f32[2,36,2]{2,1,0:T(8,128)S(1)} %get-tuple-element.40), channel_id=1, source_target_pairs={{0,1},{1,2},{2,3},{4,5},{5,6},{6,7},{8,9},{9,10},{10,11},{12,13},{... | collective-permute-start | bytes 1736 | tf_op jit(solution)/shard_map/ppermute | solution.py:22
  79.0 6.8 %collective-permute-start.19 = (f32[2,2,1024]{2,1,0:T(2,128)S(1)}, f32[2,2,1024]{2,1,0:T(2,128)S(1)}, u32[]{:S(2)}, u32[]{:S(2)}) collective-permute-start(f32[2,2,1024]{2,1,0:T(2,128)S(1)} %get-tuple-element.54), channel_id=1, source_target_pairs={{4,0},{8,4},{12,8},{16,12},{20,16},{24,20},{28,24},{5,1},{9,5},{13... | collective-permute-start | bytes 49160 | tf_op jit(solution)/shard_map/ppermute | solution.py:24
  83.8 6.5 %collective-permute-start.20 = (f32[2,2,1024]{2,1,0:T(2,128)S(1)}, f32[2,2,1024]{2,1,0:T(2,128)S(1)}, u32[]{:S(2)}, u32[]{:S(2)}) collective-permute-start(f32[2,2,1024]{2,1,0:T(2,128)S(1)} %get-tuple-element.55), channel_id=1, source_target_pairs={{0,4},{4,8},{8,12},{12,16},{16,20},{20,24},{24,28},{1,5},{5,9},{9,... | collective-permute-start | bytes 49160 | tf_op jit(solution)/shard_map/ppermute | solution.py:22
  92.7 5.3 %collective-permute-start.22 = (f32[2,36,2]{2,1,0:T(8,128)S(1)}, f32[2,36,2]{2,1,0:T(8,128)S(1)}, u32[]{:S(2)}, u32[]{:S(2)}) collective-permute-start(f32[2,36,2]{2,1,0:T(8,128)S(1)} %get-tuple-element.37), channel_id=1, source_target_pairs={{0,1},{1,2},{2,3},{4,5},{5,6},{6,7},{8,9},{9,10},{10,11},{12,13},{... | collective-permute-start | bytes 1736 | tf_op jit(solution)/shard_map/ppermute | solution.py:22
  98.8 5.9 %collective-permute-start.23 = (f32[2,2,1024]{2,1,0:T(2,128)S(1)}, f32[2,2,1024]{2,1,0:T(2,128)S(1)}, u32[]{:S(2)}, u32[]{:S(2)}) collective-permute-start(f32[2,2,1024]{2,1,0:T(2,128)S(1)} %get-tuple-element.52), channel_id=1, source_target_pairs={{4,0},{8,4},{12,8},{16,12},{20,16},{24,20},{28,24},{5,1},{9,5},{13... | collective-permute-start | bytes 49160 | tf_op jit(solution)/shard_map/ppermute | solution.py:24
  100.7 6.5 %collective-permute-start.24 = (f32[2,2,1024]{2,1,0:T(2,128)S(1)}, f32[2,2,1024]{2,1,0:T(2,128)S(1)}, u32[]{:S(2)}, u32[]{:S(2)}) collective-permute-start(f32[2,2,1024]{2,1,0:T(2,128)S(1)} %get-tuple-element.53), channel_id=1, source_target_pairs={{0,4},{4,8},{8,12},{12,16},{16,20},{20,24},{24,28},{1,5},{5,9},{9,... | collective-permute-start | bytes 49160 | tf_op jit(solution)/shard_map/ppermute | solution.py:22
  109.3 5.3 %collective-permute-start.26 = (f32[2,36,2]{2,1,0:T(8,128)S(1)}, f32[2,36,2]{2,1,0:T(8,128)S(1)}, u32[]{:S(2)}, u32[]{:S(2)}) collective-permute-start(f32[2,36,2]{2,1,0:T(8,128)S(1)} %get-tuple-element.33), channel_id=1, source_target_pairs={{0,1},{1,2},{2,3},{4,5},{5,6},{6,7},{8,9},{9,10},{10,11},{12,13},{... | collective-permute-start | bytes 1736 | tf_op jit(solution)/shard_map/ppermute | solution.py:22
  115.4 5.9 %collective-permute-start.27 = (f32[2,2,1024]{2,1,0:T(2,128)S(1)}, f32[2,2,1024]{2,1,0:T(2,128)S(1)}, u32[]{:S(2)}, u32[]{:S(2)}) collective-permute-start(f32[2,2,1024]{2,1,0:T(2,128)S(1)} %get-tuple-element.50), channel_id=1, source_target_pairs={{4,0},{8,4},{12,8},{16,12},{20,16},{24,20},{28,24},{5,1},{9,5},{13... | collective-permute-start | bytes 49160 | tf_op jit(solution)/shard_map/ppermute | solution.py:24
  118.3 6.5 %collective-permute-start.28 = (f32[2,2,1024]{2,1,0:T(2,128)S(1)}, f32[2,2,1024]{2,1,0:T(2,128)S(1)}, u32[]{:S(2)}, u32[]{:S(2)}) collective-permute-start(f32[2,2,1024]{2,1,0:T(2,128)S(1)} %get-tuple-element.51), channel_id=1, source_target_pairs={{0,4},{4,8},{8,12},{12,16},{16,20},{20,24},{24,28},{1,5},{5,9},{9,... | collective-permute-start | bytes 49160 | tf_op jit(solution)/shard_map/ppermute | solution.py:22
  (15 other events, 71.1 us)
where the time goes:
time: 134 us; the launch traced here: 133 us
  starting transfers between devices  81.7 us (61%)
  waiting for transfers between devices  39.3 us (29%)
  other arithmetic  8.08 us (6%)
  local copies, waits for them, and re-layouts  3.7 us (3%)
    ppermute x14, starting transfers between devices, extended(): lax.ppermute(head, axis, [((i + 1) % count, i) for i in range(ends)])  42.6 us
    ppermute x14, starting transfers between devices, extended(): lax.ppermute(tail, axis, [(i, (i + 1) % count) for i in range(ends)])  37.1 us
    ppermute x14, waiting for transfers between devices, extended(): lax.ppermute(tail, axis, [(i, (i + 1) % count) for i in range(ends)])  21.7 us
    ppermute x14, waiting for transfers between devices, extended(): lax.ppermute(head, axis, [((i + 1) % count, i) for i in range(ends)])  17.5 us
  transfers between devices with their start and end apart: 31, of which 14 were waited for; matrix products, arithmetic and copies ran while one was open for 2% of the time, Pallas kernels for 0%

commit v1 on v0

v1 whole, which is shorter than its diff:
```python
import functools

import jax
import jax.numpy as jnp
from jax import lax
from jax.experimental import pallas as pl
from jax.experimental.pallas import tpu as pltpu
from jax.sharding import PartitionSpec as P

STEPS = 3
RIM = 2
LANES = 128
ROWS = 8
MESH = pl.DeviceIdType.MESH


def stencil_weights(velocity):
    p = jnp.maximum(velocity, 0.0)
    q = jnp.minimum(velocity, 0.0)
    pp = p * p
    qq = q * q
    return [
        0.5 * pp - 0.5 * p,
        2.0 * p - pp,
        0.5 * pp - 1.5 * p + 0.5 * qq + 1.5 * q,
        -2.0 * q - qq,
        0.5 * qq + 0.5 * q,
    ]


def kernel(
    group_wide,
    group,
    owner_ref,
    class_ref,
    speed_ref,
    slots_ref,
    row_velocity_ref,
    column_velocity_ref,
    sea_ref,
    final_ref,
    deposit_ref,
    out_ref,
    near,
    mixed,
    far,
    field,
    slope,
    grad,
    wr,
    wc,
    centre,
    sea,
    row_send,
    row_recv,
    col_send,
    col_recv,
    near_sems,
    far_sems,
    halo_send_sems,
    halo_recv_sems,
):
    layers, height, breadth = out_ref.shape
    offsets = (-2, -1, 1, 2)
    pair = 2 if group % 2 == 0 else 1
    chips = group // pair
    w = lax.axis_index("wide")
    n = lax.axis_index("narrow")
    chip = lax.div(n, pair)
    core = lax.rem(n, pair)
    blocks = [(slice(r, r + ROWS), r) for r in range(0, height, ROWS)]

    has = {
        ("row", 0): w > 0,
        ("row", 1): w < group_wide - 1,
        ("col", 0): n > 0,
        ("col", 1): n < group - 1,
    }

    barrier = pltpu.get_barrier_semaphore()
    for side in (0, 1):
        @pl.when(has["row", side])
        def _():
            pl.semaphore_signal(
                barrier, inc=1, device_id=(w + (2 * side - 1), n), device_id_type=MESH
            )
    for by in range(1, group):
        pl.semaphore_signal(
            barrier, inc=1, device_id=(w, lax.rem(n + by, group)), device_id_type=MESH
        )
    pads = jnp.zeros((ROWS, breadth), jnp.float32)
    bottom_pad = slice(height + ROWS, height + 2 * ROWS)
    for k in range(layers):
        grad[k, 0:ROWS, :] = pads
        grad[k, bottom_pad, :] = pads
    for t in range(4):
        wr[t, 0:ROWS, :] = pads
        wr[t, bottom_pad, :] = pads
    arrivals = (
        group - 1 + has["row", 0].astype(jnp.int32) + has["row", 1].astype(jnp.int32)
    )
    pl.semaphore_wait(barrier, arrivals)

    def own(device):
        return slots_ref.at[0, :, :, pl.ds(pl.multiple_of(device * breadth, LANES), breadth)]

    order = [lax.rem(chip + by, chips) for by in range(1, chips)] + [chip]

    def near_copy(step):
        partner = chip * pair + (pair - 1 - core)
        target = order[step] * pair + (pair - 1 - core)
        return pltpu.make_async_remote_copy(
            src_ref=own(target),
            dst_ref=near.at[step],
            send_sem=near_sems.at[0, step],
            recv_sem=near_sems.at[1, step],
            device_id=(w, partner),
            device_id_type=MESH,
        )

    def far_copy(step, k):
        return pltpu.make_async_remote_copy(
            src_ref=mixed.at[step, k],
            dst_ref=far.at[step, k],
            send_sem=far_sems.at[0, step, k],
            recv_sem=far_sems.at[1, step, k],
            device_id=(w, order[step] * pair + core),
            device_id_type=MESH,
        )

    if pair == 2:
        for step in range(chips):
            near_copy(step).start()
    partner_slot = chip * pair + (pair - 1 - core)

    def chosen(step, k, rows):
        start = pl.multiple_of((order[step] * pair + core) * breadth, LANES)
        value = slots_ref[0, k, rows, pl.ds(start, breadth)]
        if pair == 2:
            value = jnp.where(owner_ref[k] == n, value, near[step, k, rows, :])
        return value

    for step in range(chips - 1):
        if pair == 2:
            near_copy(step).wait_recv()
        for k in range(layers):
            for rows, _r in blocks:
                mixed[step, k, rows, :] = chosen(step, k, rows)
            far_copy(step, k).start()

    speeds = []
    for k in range(layers):
        total = 0.0
        for c in range(speed_ref.shape[0]):
            total = jnp.where(class_ref[k] == c, speed_ref[c], total)
        speeds.append(total)

    for rows, r in blocks:
        inner = slice(ROWS + r, 2 * ROWS + r)
        row_w = stencil_weights(row_velocity_ref[rows, :])
        col_w = stencil_weights(column_velocity_ref[rows, :])
        for t, offset in enumerate(offsets):
            wr[t, inner, :] = row_w[offset + 2]
            wc[t, rows, :] = col_w[offset + 2]
        centre[rows, :] = 1.0 + row_w[2] + col_w[2]
        sea[rows, :] = sea_ref[rows, :].astype(jnp.float32)

    if pair == 2:
        near_copy(chips - 1).wait_recv()
    for k in range(layers):
        for step in range(chips - 1):
            far_copy(step, k).wait_recv()
        for rows, r in blocks:
            value = chosen(chips - 1, k, rows)
            for step in range(chips - 1):
                sender = lax.rem(chip + chips - 1 - step, chips)
                value = jnp.where(
                    lax.div(owner_ref[k], pair) == sender, far[step, k, rows, :], value
                )
            field[0, k, ROWS + r : 2 * ROWS + r, :] = value

    def halo_copies(turn):
        copies = {}
        for side in (0, 1):
            by = 2 * side - 1
            copies["row", side] = pltpu.make_async_remote_copy(
                src_ref=row_send.at[turn, side],
                dst_ref=row_recv.at[turn, side],
                send_sem=halo_send_sems.at[turn, side],
                recv_sem=halo_recv_sems.at[turn, side],
                device_id=(w + by, n),
                device_id_type=MESH,
            )
            if turn < STEPS:
                edge = slice(0, LANES) if side == 0 else slice(breadth - LANES, breadth)
                source = field.at[turn, :, ROWS : ROWS + height, edge]
            else:
                source = col_send.at[turn - STEPS, side]
            copies["col", side] = pltpu.make_async_remote_copy(
                src_ref=source,
                dst_ref=col_recv.at[turn, side],
                send_sem=halo_send_sems.at[turn, 2 + side],
                recv_sem=halo_recv_sems.at[turn, 2 + side],
                device_id=(w, n + by),
                device_id_type=MESH,
            )
        return copies

    def send_halo(turn):
        for (kind, side), copy in halo_copies(turn).items():
            pl.when(has[kind, side])(copy.start)

    def receive_halo(turn):
        for (kind, side), copy in halo_copies(turn).items():
            pl.when(has[kind, 1 - side])(copy.wait_recv)

    def ghost(side, kind):
        return has[kind, 1 - side]

    for turn in range(STEPS):
        for k in range(layers):
            rim = slice(k * RIM, (k + 1) * RIM)
            row_send[turn, 0, rim, :] = field[turn, k, ROWS : ROWS + RIM, :]
            row_send[turn, 1, rim, :] = field[turn, k, ROWS + height - RIM : ROWS + height, :]
        send_halo(turn)
        receive_halo(turn)
        for k in range(layers):
            rim = slice(k * RIM, (k + 1) * RIM)
            field[turn, k, ROWS - RIM : ROWS, :] = jnp.where(
                ghost(1, "row"), row_recv[turn, 1, rim, :], 0.0
            )
            field[turn, k, ROWS + height : ROWS + height + RIM, :] = jnp.where(
                ghost(0, "row"), row_recv[turn, 0, rim, :], 0.0
            )
        for rows, r in blocks:
            above = None
            for k in range(layers):
                base = ROWS + r
                here = field[turn, k, base : base + ROWS, :]
                wide = jnp.concatenate(
                    [
                        jnp.where(ghost(1, "col"), col_recv[turn, 1, k, rows, :], 0.0),
                        here,
                        jnp.where(ghost(0, "col"), col_recv[turn, 0, k, rows, :], 0.0),
                    ],
                    axis=1,
                )
                adv = centre[rows, :] * here
                for t, o in enumerate(offsets):
                    adv += wr[t, base : base + ROWS, :] * field[turn, k, base + o : base + o + ROWS, :]
                    moved = pltpu.roll(wide, (-o) % wide.shape[1], 1)
                    adv += wc[t, rows, :] * moved[:, LANES : LANES + breadth]
                square = adv * adv
                part = 1.0 / (1.0 + square)
                slope[turn, k, rows, :] = speeds[k] * (1.0 - square) * part * part
                if turn + 1 < STEPS:
                    flux = speeds[k] * adv * part
                    left = adv - flux
                    if above is not None:
                        left = left + above
                    field[turn + 1, k, base : base + ROWS, :] = left * sea[rows, :]
                    above = flux

    for turn in range(STEPS, 2 * STEPS):
        back = turn - STEPS
        step = STEPS - 1 - back
        adjoint = final_ref if back == 0 else out_ref
        for rows, r in blocks:
            base = ROWS + r
            mask = sea[rows, :]
            below = mask * deposit_ref[rows, :]
            for k in reversed(range(layers)):
                masked = adjoint[k, rows, :] * mask
                g = masked + (below - masked) * slope[step, k, rows, :]
                below = masked
                grad[k, base : base + ROWS, :] = g
                wall = jnp.zeros((ROWS, LANES), jnp.float32)
                gathered = None
                for t, o in enumerate(offsets):
                    product = jnp.concatenate([wall, wc[t, rows, :] * g, wall], axis=1)
                    moved = pltpu.roll(product, o % product.shape[1], 1)
                    gathered = moved if gathered is None else gathered + moved
                col_send[back, 0, k, rows, :] = gathered[:, :LANES]
                col_send[back, 1, k, rows, :] = gathered[:, LANES + breadth :]
                out_ref[k, rows, :] = gathered[:, LANES : LANES + breadth] + centre[rows, :] * g
        for k in range(layers):
            rim = slice(k * RIM, (k + 1) * RIM)
            for side, signs, at in ((0, (0, 1), ROWS - RIM), (1, (2, 3), ROWS + height)):
                total = None
                for t in signs:
                    o = offsets[t]
                    spot = slice(at - o, at - o + RIM)
                    term = wr[t, spot, :] * grad[k, spot, :]
                    total = term if total is None else total + term
                row_send[turn, side, rim, :] = total
        send_halo(turn)
        for k in range(layers):
            for rows, r in blocks:
                total = out_ref[k, rows, :]
                for t, o in enumerate(offsets):
                    spot = slice(ROWS + r - o, 2 * ROWS + r - o)
                    total += wr[t, spot, :] * grad[k, spot, :]
                out_ref[k, rows, :] = total
        receive_halo(turn)
        for k in range(layers):
            rim = slice(k * RIM, (k + 1) * RIM)
            out_ref[k, 0:RIM, :] += jnp.where(
                ghost(1, "row"), row_recv[turn, 1, rim, :], 0.0
            )
            out_ref[k, height - RIM : height, :] += jnp.where(
                ghost(0, "row"), row_recv[turn, 0, rim, :], 0.0
            )
            out_ref[k, :, 0:LANES] += jnp.where(
                ghost(1, "col"), col_recv[turn, 1, k], 0.0
            )
            out_ref[k, :, breadth - LANES : breadth] += jnp.where(
                ghost(0, "col"), col_recv[turn, 0, k], 0.0
            )

    if pair == 2:
        for step in range(chips):
            near_copy(step).wait_send()
    for step in range(chips - 1):
        for k in range(layers):
            far_copy(step, k).wait_send()
    for turn in range(2 * STEPS):
        for (kind, side), copy in halo_copies(turn).items():
            pl.when(has[kind, side])(copy.wait_send)


def body(group_wide, group, slots, owner, row_v, col_v, land_sea, layer_class, speed, final, deposit):
    layers, height, breadth = final.shape
    pair = 2 if group % 2 == 0 else 1
    chips = group // pair
    f32 = jnp.float32
    padded = height + 2 * ROWS
    vmem = pl.BlockSpec(memory_space=pltpu.VMEM)
    smem = pl.BlockSpec(memory_space=pltpu.SMEM)
    turns = 2 * STEPS
    return pl.pallas_call(
        functools.partial(kernel, group_wide, group),
        out_shape=jax.ShapeDtypeStruct(final.shape, f32),
        in_specs=[smem] * 3 + [vmem] * 6,
        out_specs=vmem,
        scratch_shapes=[
            pltpu.VMEM((chips, layers, height, breadth), f32),
            pltpu.VMEM((max(chips - 1, 1), layers, height, breadth), f32),
            pltpu.VMEM((max(chips - 1, 1), layers, height, breadth), f32),
            pltpu.VMEM((STEPS, layers, padded, breadth), f32),
            pltpu.VMEM((STEPS, layers, height, breadth), f32),
            pltpu.VMEM((layers, padded, breadth), f32),
            pltpu.VMEM((4, padded, breadth), f32),
            pltpu.VMEM((4, height, breadth), f32),
            pltpu.VMEM((height, breadth), f32),
            pltpu.VMEM((height, breadth), f32),
            pltpu.VMEM((turns, 2, layers * RIM, breadth), f32),
            pltpu.VMEM((turns, 2, layers * RIM, breadth), f32),
            pltpu.VMEM((STEPS, 2, layers, height, LANES), f32),
            pltpu.VMEM((turns, 2, layers, height, LANES), f32),
            pltpu.SemaphoreType.DMA((2, chips)),
            pltpu.SemaphoreType.DMA((2, max(chips - 1, 1), layers)),
            pltpu.SemaphoreType.DMA((turns, 4)),
            pltpu.SemaphoreType.DMA((turns, 4)),
        ],
        compiler_params=pltpu.CompilerParams(
            collective_id=0, has_side_effects=True, vmem_limit_bytes=48 * 1024 * 1024
        ),
    )(owner, layer_class, speed, slots, row_v, col_v, land_sea, final, deposit)


def solution(mesh):
    in_specs = (
        P("narrow", None, "wide", None),
        P(),
        P("wide", "narrow"),
        P("wide", "narrow"),
        P("wide", "narrow"),
        P(),
        P(),
        P(None, "wide", "narrow"),
        P("wide", "narrow"),
    )
    out_specs = P(None, "wide", "narrow")
    return jax.shard_map(
        functools.partial(body, mesh.shape["wide"], mesh.shape["narrow"]),
        mesh=mesh,
        in_specs=in_specs,
        out_specs=out_specs,
        check_vma=False,
    )
```

time: 134 us -> 43.9 us (0.33)
  the two profiles are of different devices: /device:TPU:18 before, /device:TPU:0 now
where the time goes in v1:
time: 43.9 us; the launch traced here: 43.6 us
  Pallas kernels  35.2 us (80%)
  local copies, waits for them, and re-layouts  8.46 us (19%)
    pallas_call x1, Pallas kernels, body(): pl.pallas_call(functools.partial(kernel, group_wide, group), out_shape=ja...  35.2 us
    unnamed x19, local copies, waits for them, and re-layouts  8.46 us

profile of v1, /device:TPU:0, one launch (start us, length us, event | category | flops | bytes accessed | tf_op | source)
XLA Modules:
  0.0 43.6 jit_solution(4648611195493032329)
XLA Ops:
  0.0 0.0 copy-start
  0.0 1.2 %copy-done = f32[1,2,32,4096]{3,2,1,0:T(8,128)S(1)} copy-done((f32[1,2,32,4096]{3,2,1,0:T(8,128)S(1)}, f32[1,2,32,4096]{3,2,1,0:T(8,128)}, u32[]{:S(2)}) %copy-start) | copy-done | bytes 1048600
  1.2 0.0 copy-start.1
  1.2 0.9 %copy-done.1 = f32[2,32,1024]{2,1,0:T(8,128)S(1)} copy-done((f32[2,32,1024]{2,1,0:T(8,128)S(1)}, f32[2,32,1024]{2,1,0:T(8,128)}, u32[]{:S(2)}) %copy-start.1) | copy-done | bytes 262168
  2.2 0.0 copy-start.2
  2.2 0.9 %copy-done.2 = f32[32,1024]{1,0:T(8,128)S(1)} copy-done((f32[32,1024]{1,0:T(8,128)S(1)}, f32[32,1024]{1,0:T(8,128)}, u32[]{:S(2)}) %copy-start.2) | copy-done | bytes 131096
  3.1 0.0 copy-start.3
  3.1 0.9 %copy-done.3 = f32[32,1024]{1,0:T(8,128)S(1)} copy-done((f32[32,1024]{1,0:T(8,128)S(1)}, f32[32,1024]{1,0:T(8,128)}, u32[]{:S(2)}) %copy-start.3) | copy-done | bytes 131096
  4.0 0.0 copy-start.4
  4.0 0.9 %copy-done.4 = s32[32,1024]{1,0:T(8,128)S(1)} copy-done((s32[32,1024]{1,0:T(8,128)S(1)}, s32[32,1024]{1,0:T(8,128)}, u32[]{:S(2)}) %copy-start.4) | copy-done | bytes 131096
  4.9 0.0 copy-start.5
  4.9 0.9 %copy-done.5 = f32[32,1024]{1,0:T(8,128)S(1)} copy-done((f32[32,1024]{1,0:T(8,128)S(1)}, f32[32,1024]{1,0:T(8,128)}, u32[]{:S(2)}) %copy-start.5) | copy-done | bytes 131096
  5.8 0.0 copy-start.6
  5.8 0.7 %copy-done.6 = s32[2]{0:T(128)S(1)} copy-done((s32[2]{0:T(128)S(1)}, s32[2]{0:T(128)}, u32[]{:S(2)}) %copy-start.6) | copy-done | bytes 32
  6.5 0.0 copy-start.7
  6.5 0.7 %copy-done.7 = s32[2]{0:T(128)S(1)} copy-done((s32[2]{0:T(128)S(1)}, s32[2]{0:T(128)}, u32[]{:S(2)}) %copy-start.7) | copy-done | bytes 32
  7.1 0.0 copy-start.8
  7.1 0.7 %copy-done.8 = f32[4]{0:T(128)S(1)} copy-done((f32[4]{0:T(128)S(1)}, f32[4]{0:T(128)}, u32[]{:S(2)}) %copy-start.8) | copy-done | bytes 40
  7.8 35.2 %shard_map.91 = f32[2,32,1024]{2,1,0:T(8,128)S(1)} custom-call(s32[2]{0:T(128)S(1)} %copy-done.6, s32[2]{0:T(128)S(1)} %copy-done.7, f32[4]{0:T(128)S(1)} %copy-done.8, f32[1,2,32,4096]{3,2,1,0:T(8,128)S(1)} %copy-done, f32[32,1024]{1,0:T(8,128)S(1)} %copy-done.2, f32[32,1024]{1,0:T(8,128)S(1)} %copy-done.3, s32[32,1024]{1,0:T(8,128)S(1)} %copy-done.4, ...), custom_call_target="tpu_custom_call" | custom-call | tf_op jit(solution)/shard_map/pallas_call | solution.py:340
  42.9 0.7 %copy.11 = f32[2,32,1024]{2,1,0:T(8,128)} copy(f32[2,32,1024]{2,1,0:T(8,128)S(1)} %shard_map.91) | data formatting | bytes 524288
Async XLA Ops:
  0.0 1.2 %copy-start = (f32[1,2,32,4096]{3,2,1,0:T(8,128)S(1)}, f32[1,2,32,4096]{3,2,1,0:T(8,128)}, u32[]{:S(2)}) copy-start(f32[1,2,32,4096]{3,2,1,0:T(8,128)} %slots_ref.1) | copy-start | bytes 3145732
  1.2 0.9 %copy-start.1 = (f32[2,32,1024]{2,1,0:T(8,128)S(1)}, f32[2,32,1024]{2,1,0:T(8,128)}, u32[]{:S(2)}) copy-start(f32[2,32,1024]{2,1,0:T(8,128)} %final_ref.1) | copy-start | bytes 786436
  2.2 0.9 %copy-start.2 = (f32[32,1024]{1,0:T(8,128)S(1)}, f32[32,1024]{1,0:T(8,128)}, u32[]{:S(2)}) copy-start(f32[32,1024]{1,0:T(8,128)} %row_velocity_ref.1) | copy-start | bytes 393220
  3.1 0.9 %copy-start.3 = (f32[32,1024]{1,0:T(8,128)S(1)}, f32[32,1024]{1,0:T(8,128)}, u32[]{:S(2)}) copy-start(f32[32,1024]{1,0:T(8,128)} %column_velocity_ref.1) | copy-start | bytes 393220
  4.0 0.9 %copy-start.4 = (s32[32,1024]{1,0:T(8,128)S(1)}, s32[32,1024]{1,0:T(8,128)}, u32[]{:S(2)}) copy-start(s32[32,1024]{1,0:T(8,128)} %sea_ref.1) | copy-start | bytes 393220
  4.9 0.9 %copy-start.5 = (f32[32,1024]{1,0:T(8,128)S(1)}, f32[32,1024]{1,0:T(8,128)}, u32[]{:S(2)}) copy-start(f32[32,1024]{1,0:T(8,128)} %deposit_ref.1) | copy-start | bytes 393220
  5.8 0.7 %copy-start.6 = (s32[2]{0:T(128)S(1)}, s32[2]{0:T(128)}, u32[]{:S(2)}) copy-start(s32[2]{0:T(128)} %owner_ref.1) | copy-start | bytes 28
  6.5 0.7 %copy-start.7 = (s32[2]{0:T(128)S(1)}, s32[2]{0:T(128)}, u32[]{:S(2)}) copy-start(s32[2]{0:T(128)} %class_ref.1) | copy-start | bytes 28
  7.1 0.7 %copy-start.8 = (f32[4]{0:T(128)S(1)}, f32[4]{0:T(128)}, u32[]{:S(2)}) copy-start(f32[4]{0:T(128)} %speed_ref.1) | copy-start | bytes 52

commit v2 on v1

--- a/solution.py
+++ b/solution.py
@@ -31,16 +31,27 @@
 def kernel(
     group_wide,
     group,
+    owner_hbm,
+    class_hbm,
+    speed_hbm,
+    slots_ref,
+    row_velocity_hbm,
+    column_velocity_hbm,
+    sea_hbm,
+    final_hbm,
+    deposit_hbm,
+    out_ref,
     owner_ref,
     class_ref,
     speed_ref,
-    slots_ref,
     row_velocity_ref,
     column_velocity_ref,
     sea_ref,
     final_ref,
     deposit_ref,
-    out_ref,
+    mine,
+    load_sems,
+    mine_sems,
     near,
     mixed,
     far,
@@ -77,6 +88,30 @@
         ("col", 1): n < group - 1,
     }
 
+    order = [lax.rem(chip + by, chips) for by in range(1, chips)] + [chip]
+
+    def own(device):
+        return slots_ref.at[0, :, :, pl.ds(pl.multiple_of(device * breadth, LANES), breadth)]
+
+    mine_loads = [
+        pltpu.make_async_copy(own(order[step] * pair + core), mine.at[step], mine_sems.at[step])
+        for step in range(chips)
+    ]
+    loads = [
+        pltpu.make_async_copy(source, target, load_sems.at[i])
+        for i, (source, target) in enumerate(
+            [
+                (owner_hbm, owner_ref),
+                (class_hbm, class_ref),
+                (speed_hbm, speed_ref),
+                (row_velocity_hbm, row_velocity_ref),
+                (column_velocity_hbm, column_velocity_ref),
+                (sea_hbm, sea_ref),
+                (final_hbm, final_ref),
+                (deposit_hbm, deposit_ref),
+            ]
+        )
+    ]
     barrier = pltpu.get_barrier_semaphore()
     for side in (0, 1):
         @pl.when(has["row", side])
@@ -88,6 +123,11 @@
         pl.semaphore_signal(
             barrier, inc=1, device_id=(w, lax.rem(n + by, group)), device_id_type=MESH
         )
+    loads[0].start()
+    for load in mine_loads:
+        load.start()
+    for load in loads[1:]:
+        load.start()
     pads = jnp.zeros((ROWS, breadth), jnp.float32)
     bottom_pad = slice(height + ROWS, height + 2 * ROWS)
     for k in range(layers):
@@ -101,11 +141,6 @@
     )
     pl.semaphore_wait(barrier, arrivals)
 
-    def own(device):
-        return slots_ref.at[0, :, :, pl.ds(pl.multiple_of(device * breadth, LANES), breadth)]
-
-    order = [lax.rem(chip + by, chips) for by in range(1, chips)] + [chip]
-
     def near_copy(step):
         partner = chip * pair + (pair - 1 - core)
         target = order[step] * pair + (pair - 1 - core)
@@ -134,13 +169,14 @@
     partner_slot = chip * pair + (pair - 1 - core)
 
     def chosen(step, k, rows):
-        start = pl.multiple_of((order[step] * pair + core) * breadth, LANES)
-        value = slots_ref[0, k, rows, pl.ds(start, breadth)]
+        value = mine[step, k, rows, :]
         if pair == 2:
             value = jnp.where(owner_ref[k] == n, value, near[step, k, rows, :])
         return value
 
+    loads[0].wait()
     for step in range(chips - 1):
+        mine_loads[step].wait()
         if pair == 2:
             near_copy(step).wait_recv()
         for k in range(layers):
@@ -148,6 +184,8 @@
                 mixed[step, k, rows, :] = chosen(step, k, rows)
             far_copy(step, k).start()
 
+    for load in loads[1:]:
+        load.wait()
     speeds = []
     for k in range(layers):
         total = 0.0
@@ -165,6 +203,7 @@
         centre[rows, :] = 1.0 + row_w[2] + col_w[2]
         sea[rows, :] = sea_ref[rows, :].astype(jnp.float32)
 
+    mine_loads[chips - 1].wait()
     if pair == 2:
         near_copy(chips - 1).wait_recv()
     for k in range(layers):
@@ -335,14 +374,25 @@
     f32 = jnp.float32
     padded = height + 2 * ROWS
     vmem = pl.BlockSpec(memory_space=pltpu.VMEM)
-    smem = pl.BlockSpec(memory_space=pltpu.SMEM)
+    hbm = pl.BlockSpec(memory_space=pltpu.HBM)
     turns = 2 * STEPS
     return pl.pallas_call(
         functools.partial(kernel, group_wide, group),
         out_shape=jax.ShapeDtypeStruct(final.shape, f32),
-        in_specs=[smem] * 3 + [vmem] * 6,
+        in_specs=[hbm] * 9,
         out_specs=vmem,
         scratch_shapes=[
+            pltpu.SMEM(owner.shape, owner.dtype),
+            pltpu.SMEM(layer_class.shape, layer_class.dtype),
+            pltpu.SMEM(speed.shape, speed.dtype),
+            pltpu.VMEM(row_v.shape, f32),
+            pltpu.VMEM(col_v.shape, f32),
+            pltpu.VMEM(land_sea.shape, land_sea.dtype),
+            pltpu.VMEM(final.shape, f32),
+            pltpu.VMEM(deposit.shape, f32),
+            pltpu.VMEM((chips, layers, height, breadth), f32),
+            pltpu.SemaphoreType.DMA((8,)),
+            pltpu.SemaphoreType.DMA((chips,)),
             pltpu.VMEM((chips, layers, height, breadth), f32),
             pltpu.VMEM((max(chips - 1, 1), layers, height, breadth), f32),
             pltpu.VMEM((max(chips - 1, 1), layers, height, breadth), f32),
@@ -363,7 +413,7 @@
             pltpu.SemaphoreType.DMA((turns, 4)),
         ],
         compiler_params=pltpu.CompilerParams(
-            collective_id=0, has_side_effects=True, vmem_limit_bytes=48 * 1024 * 1024
+            collective_id=0, has_side_effects=True, vmem_limit_bytes=67043328
         ),
     )(owner, layer_class, speed, slots, row_v, col_v, land_sea, final, deposit)
 

time: 43.9 us -> 37.3 us (0.85)
  local copies, waits for them, and re-layouts: 8.46 us -> 1.67 us
    unnamed x19 -> x1, local copies, waits for them, and re-layouts: 8.46 us -> 1.67 us
where the time goes in v2:
time: 37.3 us; the launch traced here: 37.2 us
  Pallas kernels  35.5 us (95%)
  local copies, waits for them, and re-layouts  1.67 us (4%)
    pallas_call x1, Pallas kernels, body(): pl.pallas_call(functools.partial(kernel, group_wide, group), out_shape=ja...  35.5 us
    unnamed x1, local copies, waits for them, and re-layouts  1.67 us

profile of v2, /device:TPU:0, one launch (start us, length us, event | category | flops | bytes accessed | tf_op | source)
XLA Modules:
  0.0 37.2 jit_solution(4301727038280906628)
XLA Ops:
  0.0 35.5 %shard_map.91 = f32[2,32,1024]{2,1,0:T(8,128)} custom-call(s32[2]{0:T(128)} %owner_hbm.1, s32[2]{0:T(128)} %class_hbm.1, f32[4]{0:T(128)} %speed_hbm.1, f32[1,2,32,4096]{3,2,1,0:T(8,128)} %slots_ref.1, f32[32,1024]{1,0:T(8,128)} %row_velocity_hbm.1, f32[32,1024]{1,0:T(8,128)} %column_velocity_hbm.1, s32[32,1024]{1,0:T(8,128)} %sea_hbm.1, ...), custom_call_target="tpu_custom_call" | custom-call | tf_op jit(solution)/shard_map/pallas_call | solution.py:379
  35.5 1.7 %copy.11 = f32[2,32,1024]{2,1,0:T(8,128)} copy(f32[2,32,1024]{2,1,0:T(8,128)} %shard_map.91) | data formatting | bytes 524288

commit v3 on v2

--- a/solution.py
+++ b/solution.py
@@ -245,9 +245,33 @@
             )
         return copies
 
-    def send_halo(turn):
+    def send_halo(turn, which):
         for (kind, side), copy in halo_copies(turn).items():
-            pl.when(has[kind, side])(copy.start)
+            if kind == which:
+                pl.when(has[kind, side])(copy.start)
+
+    def send_field_rows(turn):
+        for k in range(layers):
+            rim = slice(k * RIM, (k + 1) * RIM)
+            row_send[turn, 0, rim, :] = field[turn, k, ROWS : ROWS + RIM, :]
+            row_send[turn, 1, rim, :] = field[turn, k, ROWS + height - RIM : ROWS + height, :]
+        send_halo(turn, "row")
+
+    def send_grad_rows(turn):
+        for k in range(layers):
+            rim = slice(k * RIM, (k + 1) * RIM)
+            for side, signs, at in ((0, (0, 1), ROWS - RIM), (1, (2, 3), ROWS + height)):
+                total = None
+                for t in signs:
+                    o = offsets[t]
+                    spot = slice(at - o, at - o + RIM)
+                    term = wr[t, spot, :] * grad[k, spot, :]
+                    total = term if total is None else total + term
+                row_send[turn, side, rim, :] = total
+        send_halo(turn, "row")
+
+    edges = blocks[:1] + blocks[1:][-1:]
+    edges_first = edges + blocks[1:-1]
 
     def receive_halo(turn):
         for (kind, side), copy in halo_copies(turn).items():
@@ -256,12 +280,9 @@
     def ghost(side, kind):
         return has[kind, 1 - side]
 
+    send_field_rows(0)
     for turn in range(STEPS):
-        for k in range(layers):
-            rim = slice(k * RIM, (k + 1) * RIM)
-            row_send[turn, 0, rim, :] = field[turn, k, ROWS : ROWS + RIM, :]
-            row_send[turn, 1, rim, :] = field[turn, k, ROWS + height - RIM : ROWS + height, :]
-        send_halo(turn)
+        send_halo(turn, "col")
         receive_halo(turn)
         for k in range(layers):
             rim = slice(k * RIM, (k + 1) * RIM)
@@ -271,7 +292,7 @@
             field[turn, k, ROWS + height : ROWS + height + RIM, :] = jnp.where(
                 ghost(0, "row"), row_recv[turn, 0, rim, :], 0.0
             )
-        for rows, r in blocks:
+        for i, (rows, r) in enumerate(edges_first):
             above = None
             for k in range(layers):
                 base = ROWS + r
@@ -299,12 +320,14 @@
                         left = left + above
                     field[turn + 1, k, base : base + ROWS, :] = left * sea[rows, :]
                     above = flux
+            if turn + 1 < STEPS and i + 1 == len(edges):
+                send_field_rows(turn + 1)
 
     for turn in range(STEPS, 2 * STEPS):
         back = turn - STEPS
         step = STEPS - 1 - back
         adjoint = final_ref if back == 0 else out_ref
-        for rows, r in blocks:
+        for i, (rows, r) in enumerate(edges_first):
             base = ROWS + r
             mask = sea[rows, :]
             below = mask * deposit_ref[rows, :]
@@ -322,17 +345,9 @@
                 col_send[back, 0, k, rows, :] = gathered[:, :LANES]
                 col_send[back, 1, k, rows, :] = gathered[:, LANES + breadth :]
                 out_ref[k, rows, :] = gathered[:, LANES : LANES + breadth] + centre[rows, :] * g
-        for k in range(layers):
-            rim = slice(k * RIM, (k + 1) * RIM)
-            for side, signs, at in ((0, (0, 1), ROWS - RIM), (1, (2, 3), ROWS + height)):
-                total = None
-                for t in signs:
-                    o = offsets[t]
-                    spot = slice(at - o, at - o + RIM)
-                    term = wr[t, spot, :] * grad[k, spot, :]
-                    total = term if total is None else total + term
-                row_send[turn, side, rim, :] = total
-        send_halo(turn)
+            if i + 1 == len(edges):
+                send_grad_rows(turn)
+        send_halo(turn, "col")
         for k in range(layers):
             for rows, r in blocks:
                 total = out_ref[k, rows, :]

time: 37.3 us -> 36.5 us (0.979)
  Pallas kernels: 35.5 us -> 34.7 us
    pallas_call x1, Pallas kernels: 35.5 us -> 34.7 us  [body(): pl.pallas_call(functools.partial(kernel, group_wide, group), out_shape=ja...]
where the time goes in v3:
time: 36.5 us; the launch traced here: 36.4 us
  Pallas kernels  34.7 us (95%)
  local copies, waits for them, and re-layouts  1.67 us (5%)
    pallas_call x1, Pallas kernels, body(): pl.pallas_call(functools.partial(kernel, group_wide, group), out_shape=ja...  34.7 us
    unnamed x1, local copies, waits for them, and re-layouts  1.67 us

profile of v3, /device:TPU:0, one launch (start us, length us, event | category | flops | bytes accessed | tf_op | source)
XLA Modules:
  0.0 36.4 jit_solution(3674778586512942910)
XLA Ops:
  0.0 34.7 %shard_map.91 = f32[2,32,1024]{2,1,0:T(8,128)} custom-call(s32[2]{0:T(128)} %owner_hbm.1, s32[2]{0:T(128)} %class_hbm.1, f32[4]{0:T(128)} %speed_hbm.1, f32[1,2,32,4096]{3,2,1,0:T(8,128)} %slots_ref.1, f32[32,1024]{1,0:T(8,128)} %row_velocity_hbm.1, f32[32,1024]{1,0:T(8,128)} %column_velocity_hbm.1, s32[32,1024]{1,0:T(8,128)} %sea_hbm.1, ...), custom_call_target="tpu_custom_call" | custom-call | tf_op jit(solution)/shard_map/pallas_call | solution.py:394
  34.7 1.7 %copy.11 = f32[2,32,1024]{2,1,0:T(8,128)} copy(f32[2,32,1024]{2,1,0:T(8,128)} %shard_map.91) | data formatting | bytes 524288
